TPU v7x, 32 devices: a whole 2x2x4 slice. The times are simulated.
32 devices in a mesh: dp: 2 (over x), ep: 16 (over y, z, core).
Axes of the slice: x: 2, y: 2, z: 4, core: 2. Of those that a mesh axis runs over, the one named last changes fastest.
Arguments:
- x: bfloat16 [2, 16, 256, 3072], P('dp', 'ep'), parts along dimension 0
- expert: int32 [2, 16, 256, 4], P('dp', 'ep'), parts along dimension 0
- slot: int32 [2, 16, 256, 4], P('dp', 'ep'), parts along dimension 0
- gate: float32 [2, 16, 256, 4], P('dp', 'ep'), parts along dimension 0
- w_gate: bfloat16 [16, 3072, 10752], P('ep')
- w_up: bfloat16 [16, 3072, 10752], P('ep')
- w_down: bfloat16 [16, 10752, 3072], P('ep')
Outputs:
- y: bfloat16 [2, 16, 256, 3072], P('dp', 'ep'), parts along dimension 0
There are 2 independent parts. A program takes and returns all parts, laid end to end along the dimension named above; an argument that names none is the same for every part.
All inputs are finite; a program needn't handle non-finite values.
Results may differ from a plain program's by a relative error of at most 0.009.
Values are sent between devices in bfloat16 or wider.
A program may use at most 2 GiB of HBM per device.

v0:
```python
import jax
import jax.numpy as jnp
from jax import lax
from jax.sharding import NamedSharding, PartitionSpec as P


def einsum(form, a, b):
    return jnp.einsum(form, a.astype(jnp.float32), b.astype(jnp.float32))


def solution(mesh):
    def placed(v, *spec):
        return lax.with_sharding_constraint(v, NamedSharding(mesh, P(*spec)))

    def step(x, expert, slot, gate, w_gate, w_up, w_down):
        experts, (tokens, top) = w_gate.shape[0], expert.shape[2:]
        slots = 5 * tokens * top // (4 * experts)
        to_expert = jax.nn.one_hot(expert, experts, dtype=jnp.bfloat16)
        to_slot = jax.nn.one_hot(slot, slots, dtype=jnp.bfloat16)
        weighted = to_expert * gate[..., None].astype(jnp.bfloat16)
        dispatch = einsum("abtke,abtkc->abtec", to_expert, to_slot).astype(jnp.bfloat16)
        combine = einsum("abtke,abtkc->abtec", weighted, to_slot).astype(jnp.bfloat16)
        z = einsum("abtec,abtd->aebcd", dispatch, x).astype(jnp.bfloat16)
        z = placed(z, "dp", None, "ep", None, None)
        z = placed(z, "dp", "ep", None, None, None)
        h = jax.nn.silu(einsum("aebcd,edf->aebcf", z, w_gate))
        h = (h * einsum("aebcd,edf->aebcf", z, w_up)).astype(jnp.bfloat16)
        out = einsum("aebcf,efd->aebcd", h, w_down).astype(jnp.bfloat16)
        out = placed(out, "dp", "ep", None, None, None)
        out = placed(out, "dp", None, "ep", None, None)
        y = einsum("abtec,aebcd->abtd", combine, out)
        return y.astype(jnp.bfloat16)

    return step
```

profile of v0, /device:TPU:11, one launch (start us, length us, event | category | flops | bytes accessed | tf_op | source)
XLA Modules:
  0.0 657.6 jit_solution(2892262235725667638)
XLA Ops:
  0.0 0.0 copy-start
  0.0 0.9 copy.3
  0.9 0.0 copy-start.2
  1.0 0.8 copy.5
  1.8 0.0 copy-done.2
  1.8 0.0 copy-start.4
  1.8 0.6 copy-done.4
  2.5 2.0 fusion.34
  4.5 0.8 copy.9
  5.3 0.0 copy-done
  5.3 2.2 convert_bitcast_fusion.1
  7.5 177.7 %all-to-all.4 = bf16[1,16,1,1,80,3072]{5,4,3,2,0,1:T(8,128)(2,1)S(1)} all-to-all(bf16[1,16,1,1,80,3072]{5,4,3,2,0,1:T(8,128)(2,1)S(1)} %convert_bitcast_fusion.1), channel_id=1, replica_groups=mesh['dp'=2,'ep'=16] {'ep'}, dimensions={1} | all-to-all | bytes 15728640 | tf_op jit(solution)/sharding_constraint;jit(solution)/sharding_constraint | solution.py:13
  185.2 94.4 %fusion.2 = f32[16,80,10752]{2,1,0:T(8,128)} fusion(bf16[1,3072,10752]{2,1,0:T(8,128)(2,1)} %param.5, bf16[1,16,1,1,80,3072]{5,4,3,2,0,1:T(8,128)(2,1)S(1)} %all-to-all.4), kind=kOutput, calls=%fused_computation.2 | convolution fusion | flops 84557168640 | bytes 128974848 | tf_op jit(solution)/aebcd,edf->aebcf/dot_general | solution.py:8
  279.6 94.5 %fusion.4 = f32[16,80,10752]{2,1,0:T(8,128)} fusion(bf16[1,3072,10752]{2,1,0:T(8,128)(2,1)} %param.4, bf16[1,16,1,1,80,3072]{5,4,3,2,0,1:T(8,128)(2,1)S(1)} %all-to-all.4), kind=kOutput, calls=%fused_computation.4 | convolution fusion | flops 84557168640 | bytes 128974848 | tf_op jit(solution)/aebcd,edf->aebcf/dot_general | solution.py:8
  374.1 0.0 copy-start.6
  374.1 0.0 copy-start.3
  374.1 0.0 copy-start.5
  374.1 0.0 copy-start.1
  374.1 99.9 %convert_bitcast_fusion = bf16[1,1,16,1,80,3072]{5,4,3,1,0,2:T(8,128)(2,1)} fusion(bf16[1,10752,3072]{2,1,0:T(8,128)(2,1)} %param.6, f32[16,80,10752]{2,1,0:T(8,128)} %fusion.2, f32[16,80,10752]{2,1,0:T(8,128)} %fusion.4), kind=kOutput, calls=%fused_computation.18 | convolution fusion | flops 84643676160 | bytes 184025088 | tf_op jit(solution)/aebcf,efd->aebcd/dot_general | solution.py:8
  474.0 5.7 all-to-all-start.1
  479.6 0.0 copy-done.6
  479.6 0.1 copy.4
  479.8 0.0 copy-done.3
  479.8 0.0 copy-done.5
  479.8 2.4 fusion.38
  482.2 0.8 copy.8
  483.1 167.9 %all-to-all-done.1 = bf16[1,1,16,1,80,3072]{5,4,3,1,0,2:T(8,128)(2,1)} async-done(((bf16[1,1,16,1,80,3072]{5,4,3,1,0,2:T(8,128)(2,1)}), bf16[1,1,16,1,80,3072]{5,4,3,1,0,2:T(8,128)(2,1)}, u32[]{:S(2)}, u32[]{:S(2)}) %all-to-all-start.1) | async-done | bytes 7864352 | tf_op jit(solution)/sharding_constraint;jit(solution)/sharding_constraint | solution.py:13
  651.0 6.6 %fusion.26 = bf16[1,1,256,3072]{3,2,1,0:T(8,128)(2,1)} fusion(bf16[1,1,16,1,80,3072]{5,4,3,1,0,2:T(8,128)(2,1)} %all-to-all-done.1, bf16[256,16,80]{0,2,1:T(8,128)(2,1)S(1)} %copy.8), kind=kOutput, calls=%fused_computation.22 | convolution fusion | flops 2014052352 | bytes 10092544 | tf_op jit(solution)/abtec,aebcd->abtd/dot_general | solution.py:8
  657.6 0.0 copy-done.1
  (1 shorter events, 0.0 us)
Async XLA Ops:
  0.0 5.3 copy-start
  0.9 0.9 copy-start.2
  1.8 0.7 copy-start.4
  374.1 105.5 %copy-start.6 = (f32[1,1,256,4]{2,3,1,0:T(4,128)S(1)}, f32[1,1,256,4]{2,3,1,0:T(4,128)}, u32[]{:S(2)}) copy-start(f32[1,1,256,4]{2,3,1,0:T(4,128)} %param.1) | copy-start | bytes 12292
  374.1 105.7 %copy-start.3 = (s32[256,4]{1,0:T(8,128)S(1)}, s32[256,4]{1,0:T(8,128)}, u32[]{:S(2)}) copy-start(s32[256,4]{1,0:T(8,128)} %copy-done.2) | copy-start | bytes 12292
  374.1 105.7 %copy-start.5 = (s32[256,4]{1,0:T(8,128)S(1)}, s32[256,4]{1,0:T(8,128)}, u32[]{:S(2)}) copy-start(s32[256,4]{1,0:T(8,128)} %copy-done.4) | copy-start | bytes 12292
  374.1 283.5 %copy-start.1 = (bf16[1,1,256,3072]{3,2,1,0:T(8,128)(2,1)S(1)}, bf16[1,1,256,3072]{3,2,1,0:T(8,128)(2,1)}, u32[]{:S(2)}) copy-start(bf16[1,1,256,3072]{3,2,1,0:T(8,128)(2,1)} %param.3) | copy-start | bytes 4718596
  474.0 177.0 %all-to-all-start.1 = ((bf16[1,1,16,1,80,3072]{5,4,3,1,0,2:T(8,128)(2,1)}), bf16[1,1,16,1,80,3072]{5,4,3,1,0,2:T(8,128)(2,1)}, u32[]{:S(2)}, u32[]{:S(2)}) async-start(bf16[1,1,16,1,80,3072]{5,4,3,1,0,2:T(8,128)(2,1)} %convert_bitcast_fusion), calls=%async_computation.1 | async-start | bytes 15728640 | tf_op jit(solution)/sharding_constraint;jit(solution)/sharding_constraint | solution.py:13
where the time goes:
time: 658 us
  matrix products  302 us (46%)
  blocking collectives  178 us (27%)
  waiting for transfers between devices  168 us (26%)
    dot_general x7, matrix products, einsum(): return jnp.einsum(form, a.astype(jnp.float32), b.astype(jnp.float32))  302 us
    another operation x1, blocking collectives, placed(): return lax.with_sharding_constraint(v, NamedSharding(mesh, P(*spec)))  178 us
    another operation x1, waiting for transfers between devices, placed(): return lax.with_sharding_constraint(v, NamedSharding(mesh, P(*spec)))  168 us
  transfers between devices with their start and end apart: 1, of which 1 were waited for; matrix products, arithmetic and copies ran while one was open for 1% of the time, Pallas kernels for 0%

commit v1 on v0

v1 whole, which is shorter than its diff:
```python
import functools

import jax
import jax.numpy as jnp
from jax import lax
from jax.experimental import pallas as pl
from jax.experimental.pallas import tpu as pltpu
from jax.sharding import PartitionSpec as P

MESH = pl.DeviceIdType.MESH
F32, BF16 = jnp.float32, jnp.bfloat16
SLOTS, TOK, D, FF = 80, 256, 3072, 10752
LAYER = 4 * SLOTS
VMEM_LIMIT = 67043328
PEERS = ((0, 1), (1, 0), (1, 1))


def place():
    e = lax.axis_index("ep")
    return e // 8, (e // 2) % 4, e % 2


def flip(v, d):
    return 1 - v if d else v


def ep_of(y, z, c):
    return y * 8 + z * 2 + c


def neighbours(z):
    return 3 + (z + 2) // 3 + (5 - z) // 3


def layer_order(z, k):
    half = z // 2
    zz = z + half * (3 - 2 * z)
    far = k // 2
    low = far * k + (1 - far) * (zz + k - 2 * zz * k)
    return low + half * (3 - 2 * low)


def slot_rows(expert, info):
    rows = (lax.broadcasted_iota(jnp.int32, (SLOTS, TOK), 0) + expert * SLOTS).astype(F32)
    return [rows == info[j : j + 1, :] for j in range(4)]


TN = 512
NT = FF // TN
NB = 3
KSPLIT = 2
EVENT, GAP = 7, 17


def up_kernel(info_ref, x_ref, wg_hbm, wu_hbm, h_hbm, info_out,
              xbuf, zbuf, stage, ibuf, wbuf, hbuf,
              wsem, hsem, ssem, rsem, xsend, xrecv, isend, irecv):
    y, z, c = place()
    q = y * 2 + c
    inward = 1 - 2 * (z // 2)
    barrier = pltpu.get_barrier_semaphore()

    def at(zz):
        return {"ep": ep_of(y, zz, c)}

    def peer(r):
        dy, dc = PEERS[r]
        return flip(y, dy), flip(c, dc)

    for r in range(3):
        yy, cc = peer(r)
        pl.semaphore_signal(barrier, inc=1, device_id={"ep": ep_of(yy, z, cc)}, device_id_type=MESH)

    @pl.when(z > 0)
    def _():
        pl.semaphore_signal(barrier, inc=1, device_id=at(z - 1), device_id_type=MESH)

    @pl.when(z < 3)
    def _():
        pl.semaphore_signal(barrier, inc=1, device_id=at(z + 1), device_id_type=MESH)

    def weights(g, start):
        t = lax.rem(g, NT)
        b = lax.rem(g, NB)
        depth = D // KSPLIT
        for m, hbm in enumerate((wg_hbm, wu_hbm)):
            for r in range(KSPLIT):
                copy = pltpu.make_async_copy(
                    hbm.at[pl.ds(r * depth, depth), pl.ds(pl.multiple_of(t * TN, TN), TN)],
                    wbuf.at[b, m, pl.ds(r * depth, depth), :],
                    wsem.at[b, m, r],
                )
                if start:
                    copy.start()
                else:
                    copy.wait()

    for g in range(NB - 1):
        weights(g, True)

    def along(src_x, src_i, slot, to, way):
        return tuple(
            pltpu.make_async_remote_copy(
                src_ref=src,
                dst_ref=dst.at[slot],
                send_sem=send.at[way, slot],
                recv_sem=recv.at[slot],
                device_id=at(to),
                device_id_type=MESH,
            )
            for src, dst, send, recv in ((src_i, ibuf, isend, irecv), (src_x, xbuf, xsend, xrecv))
        )

    def swap(slot, r):
        yy, cc = peer(r)
        return pltpu.make_async_remote_copy(
            src_ref=stage.at[slot, r],
            dst_ref=zbuf.at[slot * 4 + q],
            send_sem=ssem.at[slot, r],
            recv_sem=rsem.at[slot * 4 + q],
            device_id={"ep": ep_of(yy, z, cc)},
            device_id_type=MESH,
        )

    def swap_in(slot, r):
        yy, cc = peer(r)
        return pltpu.make_async_remote_copy(
            src_ref=stage.at[slot, r],
            dst_ref=zbuf.at[slot * 4 + yy * 2 + cc],
            send_sem=ssem.at[slot, r],
            recv_sem=rsem.at[slot * 4 + yy * 2 + cc],
            device_id={"ep": ep_of(yy, z, cc)},
            device_id_type=MESH,
        )

    def deal(slot, info, x):
        def gathered(yy, cc):
            hit = slot_rows(ep_of(yy, z, cc), info)
            pick = (hit[0] | hit[1] | hit[2] | hit[3]).astype(F32).astype(BF16)
            return jnp.dot(pick, x, preferred_element_type=F32).astype(BF16)

        for n, r in enumerate((1, 2, 0)):
            stage[slot, r] = gathered(*peer(r))
            if n:
                swap(slot, (1, 2, 0)[n - 1]).start()
        zbuf[slot * 4 + q] = gathered(y, c)
        swap(slot, 0).start()

    pl.semaphore_wait(barrier, neighbours(z))

    @pl.when(z < 3)
    def _():
        for copy in along(x_ref, info_ref, z, z + 1, 1):
            copy.start()

    @pl.when(z > 0)
    def _():
        for copy in along(x_ref, info_ref, z, z - 1, 0):
            copy.start()

    deal(z, info_ref[...], x_ref[...])

    def receive(hops):
        def side(n, deal_out):
            way = inward * (1 - 2 * n)
            slot = z - way * hops
            to = z + way
            here = (slot >= 0) & (slot < 4)

            @pl.when(here)
            def _():
                if deal_out:
                    deal(slot, ibuf[slot], xbuf[slot])
                else:
                    for copy in along(xbuf.at[slot], ibuf.at[slot], slot, z, 0):
                        copy.wait_recv()

                    @pl.when((to >= 0) & (to < 4))
                    def _():
                        for copy in along(xbuf.at[slot], ibuf.at[slot], slot, to, (way + 1) // 2):
                            copy.start()

        for deal_out in (False, True):
            def both(n, carry, deal_out=deal_out):
                side(n, deal_out)
                return carry

            lax.fori_loop(0, 2, both, 0)

    def put(g):
        k = g // NT
        t = lax.rem(g, NT)
        zl = layer_order(z, k)
        b = lax.rem(g, 2)
        return pltpu.make_async_copy(
            hbuf.at[b],
            h_hbm.at[pl.ds(pl.multiple_of(zl * LAYER, LAYER), LAYER), pl.ds(pl.multiple_of(t * TN, TN), TN)],
            hsem.at[b],
        )

    def body(g, carry):
        k = g // NT
        t = lax.rem(g, NT)
        zl = layer_order(z, k)

        @pl.when((g >= EVENT) & (lax.rem(g + GAP - EVENT, GAP) == 0) & (g <= EVENT + 2 * GAP))
        def _():
            receive((g - EVENT) // GAP + 1)

        @pl.when(t == 0)
        def _():
            for r in range(3):
                swap_in(zl, r).wait_recv()

        weights(g, False)

        @pl.when(g + NB - 1 < 4 * NT)
        def _():
            weights(g + NB - 1, True)

        @pl.when(g >= 2)
        def _():
            put(g - 2).wait()

        b = lax.rem(g, NB)
        o = lax.rem(g, 2)
        rows = zbuf[pl.ds(zl * 4, 4)].reshape(LAYER, D)
        for r in range(TN // 256):
            cols = slice(r * 256, (r + 1) * 256)
            gate = jnp.dot(rows, wbuf[b, 0, :, cols], preferred_element_type=F32)
            up = jnp.dot(rows, wbuf[b, 1, :, cols], preferred_element_type=F32)
            hbuf[o, :, cols] = (jax.nn.silu(gate) * up).astype(BF16)
        put(g).start()
        return carry

    lax.fori_loop(0, 4 * NT, body, 0)
    put(4 * NT - 2).wait()
    put(4 * NT - 1).wait()
    for slot in range(4):
        for r in range(3):
            swap(slot, r).wait_send()

        @pl.when((z >= slot) & (z < 3))
        def _():
            for copy in along(x_ref, info_ref, slot, z, 1):
                copy.wait_send()

        @pl.when((z <= slot) & (z > 0))
        def _():
            for copy in along(x_ref, info_ref, slot, z, 0):
                copy.wait_send()

        @pl.when(z != slot)
        def _():
            info_out[slot] = ibuf[slot]

        @pl.when(z == slot)
        def _():
            info_out[slot] = info_ref[...]


W = 256
NS = D // W
LAG = 2


def down_kernel(info_ref, h_hbm, wd_hbm, y_ref,
                hv, wbuf, obuf, rbuf, stage, ubuf, comb,
                hsem, wsem, osend, orecv, usend, urecv):
    y, z, c = place()
    q = y * 2 + c
    barrier = pltpu.get_barrier_semaphore()

    def at(zz):
        return {"ep": ep_of(y, zz, c)}

    for dy, dc in PEERS:
        pl.semaphore_signal(barrier, inc=1, device_id={"ep": ep_of(flip(y, dy), z, flip(c, dc))}, device_id_type=MESH)

    @pl.when(z > 0)
    def _():
        pl.semaphore_signal(barrier, inc=1, device_id=at(z - 1), device_id_type=MESH)

    @pl.when(z < 3)
    def _():
        pl.semaphore_signal(barrier, inc=1, device_id=at(z + 1), device_id_type=MESH)

    def weights(s):
        b = lax.rem(s, 2)
        return pltpu.make_async_copy(
            wd_hbm.at[:, pl.ds(pl.multiple_of(s * W, W), W)], wbuf.at[b], wsem.at[b]
        )

    def h_rows(n):
        rows = pl.ds(pl.multiple_of(n * LAYER, LAYER), LAYER)
        return pltpu.make_async_copy(h_hbm.at[rows], hv.at[rows], hsem.at[n])

    weights(0).start()
    for n in range(4):
        h_rows(n).start()
    for d in range(4):
        info = info_ref[d]
        for e in range(4):
            hit = slot_rows(ep_of(e // 2, z, e % 2), info)
            total = jnp.where(hit[0], info[4:5, :], 0.0)
            for j in range(1, 4):
                total += jnp.where(hit[j], info[4 + j : 5 + j, :], 0.0)
            comb[d, e * SLOTS : (e + 1) * SLOTS, :] = total.astype(BF16)
    pl.semaphore_wait(barrier, neighbours(z))

    def across(s, r):
        dy, dc = PEERS[r]
        yy, cc = flip(y, dy), flip(c, dc)
        return pltpu.make_async_remote_copy(
            src_ref=obuf.at[lax.rem(s, 2), yy * 2 + cc],
            dst_ref=rbuf.at[s, :, q],
            send_sem=osend.at[lax.rem(s, 2), r],
            recv_sem=orecv.at[s, q],
            device_id={"ep": ep_of(yy, z, cc)},
            device_id_type=MESH,
        )

    def across_in(s, r):
        dy, dc = PEERS[r]
        yy, cc = flip(y, dy), flip(c, dc)
        return pltpu.make_async_remote_copy(
            src_ref=obuf.at[0, 0],
            dst_ref=rbuf.at[s, :, yy * 2 + cc],
            send_sem=osend.at[0, r],
            recv_sem=orecv.at[s, yy * 2 + cc],
            device_id={"ep": ep_of(yy, z, cc)},
            device_id_type=MESH,
        )

    def hop(s, d, to, slot):
        return pltpu.make_async_remote_copy(
            src_ref=stage.at[lax.rem(s, 2), d],
            dst_ref=ubuf.at[s, slot],
            send_sem=usend.at[lax.rem(s, 2), d],
            recv_sem=urecv.at[s, slot],
            device_id=at(to),
            device_id_type=MESH,
        )

    def part(s, d):
        rows = rbuf[s, d].reshape(LAYER, W)
        return lax.dot_general(comb[d], rows, (((0,), (0,)), ((), ())), preferred_element_type=F32)

    def live(s):
        return (s >= 0) & (s < NS)

    def towards(i, d, up):
        s = i - LAG - (z if up else 3 - z)

        @pl.when(live(s) & ((z < d) if up else (z > d)))
        def _():
            total = part(s, d)

            @pl.when(s >= 2)
            def _():
                hop(s - 2, d, z, d).wait_send()

            @pl.when(z == (0 if up else 3))
            def _():
                stage[lax.rem(s, 2), d] = total.astype(BF16)

            @pl.when(z != (0 if up else 3))
            def _():
                hop(s, d, z, d).wait_recv()
                stage[lax.rem(s, 2), d] = (total + ubuf[s, d].astype(F32)).astype(BF16)

    def launch(i, d, up):
        s = i - LAG - (z if up else 3 - z)
        if up:
            @pl.when(live(s) & (z < d))
            def _():
                hop(s, d, z + 1, d).start()
        else:
            @pl.when(live(s) & (z > d + 1))
            def _():
                hop(s, d, z - 1, d).start()

            @pl.when(live(s) & (z == d + 1))
            def _():
                hop(s, d, z - 1, 4).start()

    def finish(i, d):
        s = i - LAG - max(d, 3 - d)

        @pl.when(live(s) & (z == d))
        def _():
            total = part(s, d)
            if d > 0:
                hop(s, d, z, d).wait_recv()
                total += ubuf[s, d].astype(F32)
            if d < 3:
                hop(s, d, z, 4).wait_recv()
                total += ubuf[s, 4].astype(F32)
            y_ref[:, pl.ds(pl.multiple_of(s * W, W), W)] = total.astype(BF16)

    def body(i, carry):
        @pl.when((i >= LAG) & (i < NS + LAG))
        def _():
            for r in range(3):
                across_in(i - LAG, r).wait_recv()

        steps = [(3, True), (0, False), (2, True), (1, False), (1, True), (2, False)]
        for d, up in steps:
            towards(i, d, up)
        for d, up in steps:
            launch(i, d, up)
        for d in range(4):
            finish(i, d)

        @pl.when(i < NS)
        def _():
            b = lax.rem(i, 2)
            weights(i).wait()

            @pl.when(i + 1 < NS)
            def _():
                weights(i + 1).start()

            @pl.when(i >= 2)
            def _():
                for r in range(3):
                    across(i - 2, r).wait_send()

            def rows(n, carry):
                @pl.when(i == 0)
                def _():
                    h_rows(2 * n).wait()
                    h_rows(2 * n + 1).wait()

                out = jnp.dot(
                    hv[pl.ds(pl.multiple_of(n * 2 * LAYER, LAYER), 2 * LAYER), :], wbuf[b], preferred_element_type=F32
                ).astype(BF16)
                for m in range(8):
                    obuf[b, m % 4, 2 * n + m // 4] = out[m * SLOTS : (m + 1) * SLOTS, :]
                return carry

            lax.fori_loop(0, 2, rows, 0)
            rbuf[i, :, q] = obuf[b, q]
            for r in (1, 2, 0):
                across(i, r).start()

        return carry

    lax.fori_loop(0, NS + LAG + 3, body, 0)
    for s in (NS - 2, NS - 1):
        for r in range(3):
            across(s, r).wait_send()
        for d in range(4):
            @pl.when(z != d)
            def _():
                hop(s, d, z, d).wait_send()


def any_space():
    return pl.BlockSpec(memory_space=pl.ANY)


def vmem():
    return pl.BlockSpec(memory_space=pltpu.VMEM)


def project_up(info, x, wg, wu):
    rows = 16 * SLOTS
    return pl.pallas_call(
        up_kernel,
        out_shape=(jax.ShapeDtypeStruct((rows, FF), BF16), jax.ShapeDtypeStruct((4, 8, TOK), F32)),
        in_specs=[vmem(), vmem(), any_space(), any_space()],
        out_specs=(any_space(), vmem()),
        scratch_shapes=[
            pltpu.VMEM((4, TOK, D), BF16),
            pltpu.VMEM((16, SLOTS, D), BF16),
            pltpu.VMEM((4, 3, SLOTS, D), BF16),
            pltpu.VMEM((4, 8, TOK), F32),
            pltpu.VMEM((NB, 2, D, TN), BF16),
            pltpu.VMEM((2, LAYER, TN), BF16),
            pltpu.SemaphoreType.DMA((NB, 2, KSPLIT)),
            pltpu.SemaphoreType.DMA((2,)),
            pltpu.SemaphoreType.DMA((4, 3)),
            pltpu.SemaphoreType.DMA((16,)),
            pltpu.SemaphoreType.DMA((2, 4)),
            pltpu.SemaphoreType.DMA((4,)),
            pltpu.SemaphoreType.DMA((2, 4)),
            pltpu.SemaphoreType.DMA((4,)),
        ],
        compiler_params=pltpu.CompilerParams(
            collective_id=0, has_side_effects=True, vmem_limit_bytes=VMEM_LIMIT
        ),
        cost_estimate=pl.CostEstimate(
            flops=4 * rows * D * FF, bytes_accessed=16 * D * FF + 2 * rows * FF, transcendentals=rows * FF
        ),
        name="project_up",
    )(info, x, wg, wu)


def project_down(info, h, wd):
    rows = 16 * SLOTS
    return pl.pallas_call(
        down_kernel,
        out_shape=jax.ShapeDtypeStruct((TOK, D), BF16),
        in_specs=[vmem(), any_space(), any_space()],
        out_specs=vmem(),
        scratch_shapes=[
            pltpu.VMEM((rows, FF), BF16),
            pltpu.VMEM((2, FF, W), BF16),
            pltpu.VMEM((2, 4, 4, SLOTS, W), BF16),
            pltpu.VMEM((NS, 4, 4, SLOTS, W), BF16),
            pltpu.VMEM((2, 4, TOK, W), BF16),
            pltpu.VMEM((NS, 5, TOK, W), BF16),
            pltpu.VMEM((4, LAYER, TOK), BF16),
            pltpu.SemaphoreType.DMA((4,)),
            pltpu.SemaphoreType.DMA((2,)),
            pltpu.SemaphoreType.DMA((2, 3)),
            pltpu.SemaphoreType.DMA((NS, 4)),
            pltpu.SemaphoreType.DMA((2, 4)),
            pltpu.SemaphoreType.DMA((NS, 5)),
        ],
        compiler_params=pltpu.CompilerParams(
            collective_id=1, has_side_effects=True, vmem_limit_bytes=VMEM_LIMIT
        ),
        cost_estimate=pl.CostEstimate(
            flops=2 * rows * D * FF, bytes_accessed=2 * D * FF + 2 * rows * FF, transcendentals=0
        ),
        name="project_down",
    )(info, h, wd)


def solution(mesh):
    def step(x, expert, slot, gate, wg, wu, wd):
        where = jnp.where(slot[0, 0] < SLOTS, expert[0, 0] * SLOTS + slot[0, 0], -1).astype(F32)
        info = jnp.concatenate([where.T, gate[0, 0].T], axis=0)
        h, infos = project_up(info, x[0, 0], wg[0], wu[0])
        return project_down(infos, h, wd[0])[None, None]

    tokens = P("dp", "ep")
    experts = P("ep")
    return jax.shard_map(
        step,
        mesh=mesh,
        in_specs=(tokens, tokens, tokens, tokens, experts, experts, experts),
        out_specs=tokens,
        check_vma=False,
    )
```

time: 658 us -> 372 us (0.57)
  Pallas kernels: 0 us -> 361 us
  matrix products: 302 us -> 0 us
  blocking collectives: 178 us -> 0 us
  waiting for transfers between devices: 168 us -> 0 us
    pallas_call x0 -> x2, Pallas kernels: none -> 361 us  [the longest x1 223 us: project_up(): pl.pallas_call(up_kernel, out_shape=(jax.ShapeDtypeStruct((rows, FF), BF1...]
    dot_general x7 -> x0, matrix products: 302 us -> none  [einsum(): return jnp.einsum(form, a.astype(jnp.float32), b.astype(jnp.float32))]
    another operation x1 -> x0, blocking collectives: 178 us -> none  [placed(): return lax.with_sharding_constraint(v, NamedSharding(mesh, P(*spec)))]
    another operation x1 -> x0, waiting for transfers between devices: 168 us -> none  [placed(): return lax.with_sharding_constraint(v, NamedSharding(mesh, P(*spec)))]
  transfers between devices with their start and end apart: 1 -> 0, of which waited for: 1 -> 0; matrix products, arithmetic and copies ran while one was open for 1% -> 0% of each run, Pallas kernels for 0% -> 0%
where the time goes in v1:
time: 372 us; the launch traced here: 366 us
  Pallas kernels  361 us (97%)
    pallas_call x1, Pallas kernels, project_up(): pl.pallas_call(up_kernel, out_shape=(jax.ShapeDtypeStruct((rows, FF), BF1...  223 us
    pallas_call x1, Pallas kernels, project_down(): pl.pallas_call(down_kernel, out_shape=jax.ShapeDtypeStruct((TOK, D), BF16...  138 us

profile of v1, /device:TPU:11, one launch (start us, length us, event | category | flops | bytes accessed | tf_op | source)
XLA Modules:
  0.0 365.9 jit_solution(14873772113367728005)
XLA Ops:
  0.0 0.7 convert_bitcast_fusion
  0.7 1.3 pad_maximum_fusion.info_ref
  2.0 222.9 %project_up.1 = (bf16[1280,10752]{1,0:T(8,128)(2,1)}, f32[4,8,256]{2,1,0:T(8,128)}) custom-call(f32[8,256]{1,0:T(8,128)} %pad_maximum_fusion.info_ref, bf16[256,3072]{1,0:T(8,128)(2,1)} %bitcast.17, bf16[3072,10752]{1,0:T(8,128)(2,1)} %bitcast.14, bf16[3072,10752]{1,0:T(8,128)(2,1)} %bitcast.15), custom_call_target="tpu_custom_call" | custom-call | flops 169114337280 | bytes 556007424 | tf_op jit(solution)/shard_map/project_up/pallas_call | solution.py:469
  224.9 138.4 %project_down.1 = bf16[256,3072]{1,0:T(8,128)(2,1)} custom-call(f32[4,8,256]{2,1,0:T(8,128)} %get-tuple-element.7.info_ref, bf16[1280,10752]{1,0:T(8,128)(2,1)} %get-tuple-element.8.h_hbm, bf16[10752,3072]{1,0:T(8,128)(2,1)} %bitcast.16), custom_call_target="tpu_custom_call" | custom-call | flops 84557168640 | bytes 93585408 | tf_op jit(solution)/shard_map/project_down/pallas_call | solution.py:502
  363.3 2.7 copy.9

commit v2 on v1

--- a/solution.py
+++ b/solution.py
@@ -47,9 +47,11 @@
 
 TN = 512
 NT = FF // TN
-NB = 3
+NB = 4
 KSPLIT = 2
-EVENT, GAP = 7, 17
+HEAD = 10
+DEAL = 512
+EVENT, GAP = 18, 16
 
 
 def up_kernel(info_ref, x_ref, wg_hbm, wu_hbm, h_hbm, info_out,
@@ -134,17 +136,19 @@
         )
 
     def deal(slot, info, x):
-        def gathered(yy, cc):
+        def pick(yy, cc):
             hit = slot_rows(ep_of(yy, z, cc), info)
-            pick = (hit[0] | hit[1] | hit[2] | hit[3]).astype(F32).astype(BF16)
-            return jnp.dot(pick, x, preferred_element_type=F32).astype(BF16)
-
-        for n, r in enumerate((1, 2, 0)):
-            stage[slot, r] = gathered(*peer(r))
-            if n:
-                swap(slot, (1, 2, 0)[n - 1]).start()
-        zbuf[slot * 4 + q] = gathered(y, c)
-        swap(slot, 0).start()
+            return (hit[0] | hit[1] | hit[2] | hit[3]).astype(F32).astype(BF16)
+
+        picks = jnp.concatenate([pick(*peer(r)) for r in (1, 2, 0)] + [pick(y, c)], axis=0)
+        for n in range(D // DEAL):
+            cols = slice(n * DEAL, (n + 1) * DEAL)
+            rows = jnp.dot(picks, x[:, cols], preferred_element_type=F32).astype(BF16)
+            for m, r in enumerate((1, 2, 0)):
+                stage[slot, r, :, cols] = rows[m * SLOTS : (m + 1) * SLOTS, :]
+            zbuf[slot * 4 + q, :, cols] = rows[3 * SLOTS :, :]
+        for r in (1, 2, 0):
+            swap(slot, r).start()
 
     pl.semaphore_wait(barrier, neighbours(z))
 
@@ -158,7 +162,7 @@
         for copy in along(x_ref, info_ref, z, z - 1, 0):
             copy.start()
 
-    deal(z, info_ref[...], x_ref[...])
+    deal(z, info_ref[...], x_ref)
 
     def receive(hops):
         def side(n, deal_out):
@@ -170,7 +174,7 @@
             @pl.when(here)
             def _():
                 if deal_out:
-                    deal(slot, ibuf[slot], xbuf[slot])
+                    deal(slot, ibuf[slot], xbuf.at[slot])
                 else:
                     for copy in along(xbuf.at[slot], ibuf.at[slot], slot, z, 0):
                         copy.wait_recv()
@@ -187,21 +191,55 @@
 
             lax.fori_loop(0, 2, both, 0)
 
-    def put(g):
+    def plan(g):
         k = g // NT
         t = lax.rem(g, NT)
         zl = layer_order(z, k)
+        head = (NT - 1 - t) // (NT - HEAD)
+        start = (3 - k) // 3
+        before = layer_order(z, k - 1 + start)
+        other = zl + head * (1 - start) * (before - zl)
+        pieces = (
+            other * 4 + (1 - y) * 2,
+            zl * 4 + y * 2,
+            zl * 4 + (start * y + (1 - start) * (1 - y)) * 2,
+        )
+        pair = (k > 0) | (t >= HEAD)
+        lone = ((k == 0) | (k == 3)) & (t < HEAD)
+        return k, t, zl, pieces, pair, lone
+
+    def put(g, wait):
+        k, t, zl, pieces, pair, lone = plan(g)
         b = lax.rem(g, 2)
-        return pltpu.make_async_copy(
-            hbuf.at[b],
-            h_hbm.at[pl.ds(pl.multiple_of(zl * LAYER, LAYER), LAYER), pl.ds(pl.multiple_of(t * TN, TN), TN)],
-            hsem.at[b],
-        )
+        copies = [
+            pltpu.make_async_copy(
+                hbuf.at[b, n],
+                h_hbm.at[
+                    pl.ds(pl.multiple_of(pieces[n] * SLOTS, 2 * SLOTS), 2 * SLOTS),
+                    pl.ds(pl.multiple_of(t * TN, TN), TN),
+                ],
+                hsem.at[b, n],
+            )
+            for n in range(3)
+        ]
+
+        def each(chosen):
+            for copy in chosen:
+                if wait:
+                    copy.wait()
+                else:
+                    copy.start()
+
+        @pl.when(pair)
+        def _():
+            each(copies[:2])
+
+        @pl.when(lone)
+        def _():
+            each(copies[2:])
 
     def body(g, carry):
-        k = g // NT
-        t = lax.rem(g, NT)
-        zl = layer_order(z, k)
+        k, t, zl, pieces, pair, lone = plan(g)
 
         @pl.when((g >= EVENT) & (lax.rem(g + GAP - EVENT, GAP) == 0) & (g <= EVENT + 2 * GAP))
         def _():
@@ -209,8 +247,12 @@
 
         @pl.when(t == 0)
         def _():
-            for r in range(3):
-                swap_in(zl, r).wait_recv()
+            swap_in(zl, 0).wait_recv()
+
+        @pl.when(((t == HEAD) & (k < 3)) | ((t == 0) & (k == 3)))
+        def _():
+            swap_in(zl, 1).wait_recv()
+            swap_in(zl, 2).wait_recv()
 
         weights(g, False)
 
@@ -220,22 +262,41 @@
 
         @pl.when(g >= 2)
         def _():
-            put(g - 2).wait()
+            put(g - 2, True)
 
         b = lax.rem(g, NB)
         o = lax.rem(g, 2)
-        rows = zbuf[pl.ds(zl * 4, 4)].reshape(LAYER, D)
-        for r in range(TN // 256):
-            cols = slice(r * 256, (r + 1) * 256)
-            gate = jnp.dot(rows, wbuf[b, 0, :, cols], preferred_element_type=F32)
-            up = jnp.dot(rows, wbuf[b, 1, :, cols], preferred_element_type=F32)
-            hbuf[o, :, cols] = (jax.nn.silu(gate) * up).astype(BF16)
-        put(g).start()
+
+        def project(rows, outs):
+            for r in range(TN // 256):
+                cols = slice(r * 256, (r + 1) * 256)
+                gate = jnp.dot(rows, wbuf[b, 0, :, cols], preferred_element_type=F32)
+                up = jnp.dot(rows, wbuf[b, 1, :, cols], preferred_element_type=F32)
+                h = (jax.nn.silu(gate) * up).astype(BF16)
+                for m, n in enumerate(outs):
+                    hbuf[o, n, :, cols] = h[m * 2 * SLOTS : (m + 1) * 2 * SLOTS, :]
+
+        def held(n):
+            return zbuf[pl.ds(pieces[n], 2)].reshape(2 * SLOTS, D)
+
+        @pl.when(pair & jnp.logical_not(lone))
+        def _():
+            project(jnp.concatenate([held(0), held(1)], axis=0), (0, 1))
+
+        @pl.when(pair & lone)
+        def _():
+            project(jnp.concatenate([held(0), held(1), held(2)], axis=0), (0, 1, 2))
+
+        @pl.when(lone & (k == 0))
+        def _():
+            project(held(2), (2,))
+
+        put(g, False)
         return carry
 
     lax.fori_loop(0, 4 * NT, body, 0)
-    put(4 * NT - 2).wait()
-    put(4 * NT - 1).wait()
+    put(4 * NT - 2, True)
+    put(4 * NT - 1, True)
     for slot in range(4):
         for r in range(3):
             swap(slot, r).wait_send()
@@ -261,7 +322,9 @@
 
 W = 256
 NS = D // W
-LAG = 2
+KEEP = 6
+SKEW = 6
+LATE = 5
 
 
 def down_kernel(info_ref, h_hbm, wd_hbm, y_ref,
@@ -269,13 +332,23 @@
                 hsem, wsem, osend, orecv, usend, urecv):
     y, z, c = place()
     q = y * 2 + c
+    near = z // 2 * 2
+    far = 2 - near
+    inner = z * (3 - z) // 2
+    onward = z + 1 - near
+    other = 2 * near + 1 - z
     barrier = pltpu.get_barrier_semaphore()
 
     def at(zz):
         return {"ep": ep_of(y, zz, c)}
 
-    for dy, dc in PEERS:
-        pl.semaphore_signal(barrier, inc=1, device_id={"ep": ep_of(flip(y, dy), z, flip(c, dc))}, device_id_type=MESH)
+    def peer(r):
+        dy, dc = PEERS[r]
+        return flip(y, dy), flip(c, dc)
+
+    for r in range(3):
+        yy, cc = peer(r)
+        pl.semaphore_signal(barrier, inc=1, device_id={"ep": ep_of(yy, z, cc)}, device_id_type=MESH)
 
     @pl.when(z > 0)
     def _():
@@ -285,8 +358,9 @@
     def _():
         pl.semaphore_signal(barrier, inc=1, device_id=at(z + 1), device_id_type=MESH)
 
-    def weights(s):
-        b = lax.rem(s, 2)
+    def weights(i):
+        b = lax.rem(i, 2)
+        s = lax.rem(i, NS)
         return pltpu.make_async_copy(
             wd_hbm.at[:, pl.ds(pl.multiple_of(s * W, W), W)], wbuf.at[b], wsem.at[b]
         )
@@ -296,8 +370,8 @@
         return pltpu.make_async_copy(h_hbm.at[rows], hv.at[rows], hsem.at[n])
 
     weights(0).start()
-    for n in range(4):
-        h_rows(n).start()
+    for n in range(2):
+        h_rows(far + n).start()
     for d in range(4):
         info = info_ref[d]
         for e in range(4):
@@ -308,116 +382,134 @@
             comb[d, e * SLOTS : (e + 1) * SLOTS, :] = total.astype(BF16)
     pl.semaphore_wait(barrier, neighbours(z))
 
-    def across(s, r):
-        dy, dc = PEERS[r]
-        yy, cc = flip(y, dy), flip(c, dc)
+    def across(i, r):
+        yy, cc = peer(r)
+        half = i // NS
+        base = far + half * (near - far)
+        s = i - half * NS
         return pltpu.make_async_remote_copy(
-            src_ref=obuf.at[lax.rem(s, 2), yy * 2 + cc],
-            dst_ref=rbuf.at[s, :, q],
-            send_sem=osend.at[lax.rem(s, 2), r],
-            recv_sem=orecv.at[s, q],
+            src_ref=obuf.at[lax.rem(i, 2), yy * 2 + cc],
+            dst_ref=rbuf.at[s, pl.ds(base, 2), q],
+            send_sem=osend.at[lax.rem(i, 2), r],
+            recv_sem=orecv.at[s, q, half],
             device_id={"ep": ep_of(yy, z, cc)},
             device_id_type=MESH,
         )
 
-    def across_in(s, r):
-        dy, dc = PEERS[r]
-        yy, cc = flip(y, dy), flip(c, dc)
+    def across_in(s, r, half):
+        yy, cc = peer(r)
+        base = near if half else far
         return pltpu.make_async_remote_copy(
             src_ref=obuf.at[0, 0],
-            dst_ref=rbuf.at[s, :, yy * 2 + cc],
+            dst_ref=rbuf.at[s, pl.ds(base, 2), yy * 2 + cc],
             send_sem=osend.at[0, r],
-            recv_sem=orecv.at[s, yy * 2 + cc],
+            recv_sem=orecv.at[s, yy * 2 + cc, half],
             device_id={"ep": ep_of(yy, z, cc)},
             device_id_type=MESH,
         )
 
-    def hop(s, d, to, slot):
+    def hop(s, n, to, slot):
         return pltpu.make_async_remote_copy(
-            src_ref=stage.at[lax.rem(s, 2), d],
+            src_ref=stage.at[lax.rem(s, KEEP), n],
             dst_ref=ubuf.at[s, slot],
-            send_sem=usend.at[lax.rem(s, 2), d],
+            send_sem=usend.at[lax.rem(s, KEEP), n],
             recv_sem=urecv.at[s, slot],
             device_id=at(to),
             device_id_type=MESH,
         )
 
+    def far_hop(s, n):
+        last = z // 2 * (3 - z) * n
+        d = far + n
+        return hop(s, n, onward, d + last * (4 - d))
+
+    def near_hop(s):
+        return hop(s, 2, other, other + lax.rem(z, 2) * (4 - other))
+
+    def arrived(s, slot):
+        hop(s, 2, z, slot).wait_recv()
+
+    def live(s):
+        return (s >= 0) & (s < NS)
+
+    def clamp(s):
+        w = (s + 2 * NS) // NS
+        inside = (w - 1) * (3 - w)
+        return inside * s + (1 - inside) * NS, inside
+
     def part(s, d):
         rows = rbuf[s, d].reshape(LAYER, W)
         return lax.dot_general(comb[d], rows, (((0,), (0,)), ((), ())), preferred_element_type=F32)
 
-    def live(s):
-        return (s >= 0) & (s < NS)
-
-    def towards(i, d, up):
-        s = i - LAG - (z if up else 3 - z)
-
-        @pl.when(live(s) & ((z < d) if up else (z > d)))
-        def _():
-            total = part(s, d)
-
-            @pl.when(s >= 2)
-            def _():
-                hop(s - 2, d, z, d).wait_send()
-
-            @pl.when(z == (0 if up else 3))
-            def _():
-                stage[lax.rem(s, 2), d] = total.astype(BF16)
-
-            @pl.when(z != (0 if up else 3))
-            def _():
-                hop(s, d, z, d).wait_recv()
-                stage[lax.rem(s, 2), d] = (total + ubuf[s, d].astype(F32)).astype(BF16)
-
-    def launch(i, d, up):
-        s = i - LAG - (z if up else 3 - z)
-        if up:
-            @pl.when(live(s) & (z < d))
-            def _():
-                hop(s, d, z + 1, d).start()
-        else:
-            @pl.when(live(s) & (z > d + 1))
-            def _():
-                hop(s, d, z - 1, d).start()
-
-            @pl.when(live(s) & (z == d + 1))
-            def _():
-                hop(s, d, z - 1, 4).start()
-
-    def finish(i, d):
-        s = i - LAG - max(d, 3 - d)
-
-        @pl.when(live(s) & (z == d))
-        def _():
-            total = part(s, d)
-            if d > 0:
-                hop(s, d, z, d).wait_recv()
-                total += ubuf[s, d].astype(F32)
-            if d < 3:
-                hop(s, d, z, 4).wait_recv()
-                total += ubuf[s, 4].astype(F32)
-            y_ref[:, pl.ds(pl.multiple_of(s * W, W), W)] = total.astype(BF16)
+    def far_part(s):
+        at_s, inside = clamp(s)
+        slot = inside * lax.rem(s + 2 * KEEP, KEEP) + (1 - inside) * KEEP
+        for n in range(2):
+            came = jnp.where(inner == 1, ubuf[at_s, far + n].astype(F32), 0.0)
+            stage[slot, n] = (part(at_s, far + n) + came).astype(BF16)
+
+    def near_part(s):
+        at_s, inside = clamp(s)
+        slot = inside * lax.rem(s + 2 * KEEP, KEEP) + (1 - inside) * KEEP
+        came = jnp.where(inner == 1, ubuf[at_s, other].astype(F32), 0.0)
+        stage[slot, 2] = (part(at_s, other) + came).astype(BF16)
+
+    def finish(s):
+        at_s, inside = clamp(s)
+        below = jnp.where(z > 0, ubuf[at_s, z].astype(F32), 0.0)
+        above = jnp.where(z < 3, ubuf[at_s, 4].astype(F32), 0.0)
+        total = part(at_s, z) + below + above
+        y_ref[:, pl.ds(pl.multiple_of(inside * s * W, W), W)] = total.astype(BF16)
 
     def body(i, carry):
-        @pl.when((i >= LAG) & (i < NS + LAG))
+        s_far = i - 2 - SKEW * inner
+        s_near = i - NS - 2
+        s_out = s_near - LATE
+
+        def wait_out():
+            @pl.when(live(s_out))
+            def _():
+                @pl.when(z > 0)
+                def _():
+                    arrived(s_out, z)
+
+                @pl.when(z < 3)
+                def _():
+                    arrived(s_out, 4)
+
+        @pl.when(live(s_far))
         def _():
             for r in range(3):
-                across_in(i - LAG, r).wait_recv()
-
-        steps = [(3, True), (0, False), (2, True), (1, False), (1, True), (2, False)]
-        for d, up in steps:
-            towards(i, d, up)
-        for d, up in steps:
-            launch(i, d, up)
-        for d in range(4):
-            finish(i, d)
-
-        @pl.when(i < NS)
-        def _():
+                across_in(s_far, r, 0).wait_recv()
+            for n in range(2):
+                @pl.when(inner == 1)
+                def _(n=n):
+                    arrived(s_far, far + n)
+
+                @pl.when(s_far >= KEEP)
+                def _(n=n):
+                    far_hop(s_far - KEEP, n).wait_send()
+
+        @pl.when(live(s_near))
+        def _():
+            for r in range(3):
+                across_in(s_near, r, 1).wait_recv()
+
+            @pl.when(inner == 1)
+            def _():
+                arrived(s_near, other)
+
+            @pl.when(s_near >= KEEP)
+            def _():
+                near_hop(s_near - KEEP).wait_send()
+
+        @pl.when(i < 2 * NS)
+        def _():
+            wait_out()
             b = lax.rem(i, 2)
             weights(i).wait()
 
-            @pl.when(i + 1 < NS)
+            @pl.when(i + 1 < 2 * NS)
             def _():
                 weights(i + 1).start()
 
@@ -426,34 +518,71 @@
                 for r in range(3):
                     across(i - 2, r).wait_send()
 
-            def rows(n, carry):
-                @pl.when(i == 0)
-                def _():
-                    h_rows(2 * n).wait()
-                    h_rows(2 * n + 1).wait()
-
+            @pl.when(i == 0)
+            def _():
+                for n in range(2):
+                    h_rows(far + n).wait()
+                for n in range(2):
+                    h_rows(near + n).start()
+
+            @pl.when(i == NS)
+            def _():
+                for n in range(2):
+                    h_rows(near + n).wait()
+
+            def rows(base):
                 out = jnp.dot(
-                    hv[pl.ds(pl.multiple_of(n * 2 * LAYER, LAYER), 2 * LAYER), :], wbuf[b], preferred_element_type=F32
+                    hv[pl.ds(pl.multiple_of(base * LAYER, 2 * LAYER), 2 * LAYER), :],
+                    wbuf[b],
+                    preferred_element_type=F32,
                 ).astype(BF16)
                 for m in range(8):
-                    obuf[b, m % 4, 2 * n + m // 4] = out[m * SLOTS : (m + 1) * SLOTS, :]
-                return carry
-
-            lax.fori_loop(0, 2, rows, 0)
-            rbuf[i, :, q] = obuf[b, q]
+                    obuf[b, m % 4, m // 4] = out[m * SLOTS : (m + 1) * SLOTS, :]
+                far_part(s_far)
+
+            @pl.when(i < NS)
+            def _():
+                rows(far)
+                rbuf[i, pl.ds(far, 2), q] = obuf[b, q]
+
+            @pl.when(i >= NS)
+            def _():
+                rows(near)
+                near_part(s_near)
+                finish(s_out)
+                rbuf[i - NS, pl.ds(near, 2), q] = obuf[b, q]
+
             for r in (1, 2, 0):
                 across(i, r).start()
 
+        @pl.when(live(s_far))
+        def _():
+            for n in (1, 0):
+                far_hop(s_far, n).start()
+
+        @pl.when((i >= 2 * NS) & live(s_near))
+        def _():
+            near_part(s_near)
+
+        @pl.when(live(s_near))
+        def _():
+            near_hop(s_near).start()
+
+        @pl.when((i >= 2 * NS) & live(s_out))
+        def _():
+            wait_out()
+            finish(s_out)
+
         return carry
 
-    lax.fori_loop(0, NS + LAG + 3, body, 0)
-    for s in (NS - 2, NS - 1):
+    lax.fori_loop(0, 2 * NS + 2 + LATE, body, 0)
+    for i in (2 * NS - 2, 2 * NS - 1):
         for r in range(3):
-            across(s, r).wait_send()
-        for d in range(4):
-            @pl.when(z != d)
-            def _():
-                hop(s, d, z, d).wait_send()
+            across(i, r).wait_send()
+    for s in range(NS - KEEP, NS):
+        for n in range(2):
+            far_hop(s, n).wait_send()
+        near_hop(s).wait_send()
 
 
 def any_space():
@@ -477,9 +606,9 @@
             pltpu.VMEM((4, 3, SLOTS, D), BF16),
             pltpu.VMEM((4, 8, TOK), F32),
             pltpu.VMEM((NB, 2, D, TN), BF16),
-            pltpu.VMEM((2, LAYER, TN), BF16),
+            pltpu.VMEM((2, 3, 2 * SLOTS, TN), BF16),
             pltpu.SemaphoreType.DMA((NB, 2, KSPLIT)),
-            pltpu.SemaphoreType.DMA((2,)),
+            pltpu.SemaphoreType.DMA((2, 3)),
             pltpu.SemaphoreType.DMA((4, 3)),
             pltpu.SemaphoreType.DMA((16,)),
             pltpu.SemaphoreType.DMA((2, 4)),
@@ -507,16 +636,16 @@
         scratch_shapes=[
             pltpu.VMEM((rows, FF), BF16),
             pltpu.VMEM((2, FF, W), BF16),
-            pltpu.VMEM((2, 4, 4, SLOTS, W), BF16),
-            pltpu.VMEM((NS, 4, 4, SLOTS, W), BF16),
-            pltpu.VMEM((2, 4, TOK, W), BF16),
-            pltpu.VMEM((NS, 5, TOK, W), BF16),
+            pltpu.VMEM((2, 4, 2, SLOTS, W), BF16),
+            pltpu.VMEM((NS + 1, 4, 4, SLOTS, W), BF16),
+            pltpu.VMEM((KEEP + 1, 3, TOK, W), BF16),
+            pltpu.VMEM((NS + 1, 5, TOK, W), BF16),
             pltpu.VMEM((4, LAYER, TOK), BF16),
             pltpu.SemaphoreType.DMA((4,)),
             pltpu.SemaphoreType.DMA((2,)),
             pltpu.SemaphoreType.DMA((2, 3)),
-            pltpu.SemaphoreType.DMA((NS, 4)),
-            pltpu.SemaphoreType.DMA((2, 4)),
+            pltpu.SemaphoreType.DMA((NS, 4, 2)),
+            pltpu.SemaphoreType.DMA((KEEP, 3)),
             pltpu.SemaphoreType.DMA((NS, 5)),
         ],
         compiler_params=pltpu.CompilerParams(

time: 372 us -> 351 us (0.944)
  Pallas kernels: 361 us -> 344 us
    pallas_call x1, Pallas kernels: 138 us -> 129 us  [project_down(): pl.pallas_call(down_kernel, out_shape=jax.ShapeDtypeStruct((TOK, D), BF16...]
    pallas_call x1, Pallas kernels: 223 us -> 215 us  [project_up(): pl.pallas_call(up_kernel, out_shape=(jax.ShapeDtypeStruct((rows, FF), BF1...]
where the time goes in v2:
time: 351 us; the launch traced here: 349 us
  Pallas kernels  344 us (98%)
    pallas_call x1, Pallas kernels, project_up(): pl.pallas_call(up_kernel, out_shape=(jax.ShapeDtypeStruct((rows, FF), BF1...  215 us
    pallas_call x1, Pallas kernels, project_down(): pl.pallas_call(down_kernel, out_shape=jax.ShapeDtypeStruct((TOK, D), BF16...  129 us

profile of v2, /device:TPU:11, one launch (start us, length us, event | category | flops | bytes accessed | tf_op | source)
XLA Modules:
  0.0 348.5 jit_solution(17310384835481400204)
XLA Ops:
  0.0 0.7 convert_bitcast_fusion
  0.7 1.3 pad_maximum_fusion.info_ref
  2.0 214.6 %project_up.1 = (bf16[1280,10752]{1,0:T(8,128)(2,1)}, f32[4,8,256]{2,1,0:T(8,128)}) custom-call(f32[8,256]{1,0:T(8,128)} %pad_maximum_fusion.info_ref, bf16[256,3072]{1,0:T(8,128)(2,1)} %bitcast.17, bf16[3072,10752]{1,0:T(8,128)(2,1)} %bitcast.14, bf16[3072,10752]{1,0:T(8,128)(2,1)} %bitcast.15), custom_call_target="tpu_custom_call" | custom-call | flops 169114337280 | bytes 556007424 | tf_op jit(solution)/shard_map/project_up/pallas_call | solution.py:598
  216.6 129.3 %project_down.1 = bf16[256,3072]{1,0:T(8,128)(2,1)} custom-call(f32[4,8,256]{2,1,0:T(8,128)} %get-tuple-element.7.info_ref, bf16[1280,10752]{1,0:T(8,128)(2,1)} %get-tuple-element.8.h_hbm, bf16[10752,3072]{1,0:T(8,128)(2,1)} %bitcast.16), custom_call_target="tpu_custom_call" | custom-call | flops 84557168640 | bytes 93585408 | tf_op jit(solution)/shard_map/project_down/pallas_call | solution.py:631
  345.9 2.7 copy.9
